TPU v7x, 32 devices: a whole 2x2x4 slice. The times are simulated.
32 devices in a mesh: row: 8 (over y, x, core), col: 4 (over z).
Axes of the slice: x: 2, y: 2, z: 4, core: 2. Of those that a mesh axis runs over, the one named last changes fastest.
Arguments:
- gradient: float32 [2048, 4608], P('row', 'col'), may hold values from -12 to 12
- first_moment: float32 [2048, 4608], P('row', 'col'), may hold values from -12 to 12, as said below
- second_moment: float32 [2048, 4608], P('row', 'col'), may hold values from 0.01 to 1
- weights: float32 [2048, 4608], P('row', 'col'), may hold values from -6 to 6
- eigenbasis: float32 [4608, 4608], P('row', 'col'), may hold values from -1 to 1, as said below
Outputs:
- new_weights: float32 [2048, 4608], P('row', 'col')
- new_first: float32 [2048, 4608], P('row', 'col')
- new_second: float32 [2048, 4608], P('row', 'col')
Inputs may be any that keep to these rules, and one draw needn't show every extreme that they name: `first_moment`: every entry's magnitude is at most 12. eigenbasis is orthogonal: its columns are orthonormal.
All inputs are finite; a program needn't handle non-finite values.
Results may differ from a plain program's by a relative error of at most 0.000059.
Values sent between devices are 32-bit elements; how exact they have to be, the bound alone decides.
No kernel may reach another device: no remote copies, remote signals or barrier semaphores. Data moves between devices by JAX's collectives and lax.ppermute only.
A program may use at most 64 MiB of HBM per device.

v0:
```python
import jax
import jax.numpy as jnp
from jax import lax
from jax.experimental import pallas as pl
from jax.experimental.pallas import tpu as pltpu
from jax.sharding import PartitionSpec as P


bias_first = 1.0 - 0.9**10
bias_second = 1.0 - 0.999**10
epsilon = 1e-08
step_rate = 0.25


f32, bf16 = jnp.float32, jnp.bfloat16


def plain(gradient, first_moment, second_moment, weights, eigenbasis):
    high = lax.Precision.HIGH
    slab = lax.all_gather(eigenbasis, "row", axis=0, tiled=True)
    whole = lax.all_gather(gradient, "col", axis=1, tiled=True)
    rotated = jnp.dot(whole, slab, precision=high, preferred_element_type=f32)
    new_first = 0.9 * first_moment + 0.1 * rotated
    new_second = 0.999 * second_moment + 0.001 * rotated * rotated
    direction = new_first / bias_first / (jnp.sqrt(new_second / bias_second) + epsilon)
    sum_squares = lax.psum(jnp.sum(direction * direction, axis=1), "col")
    part = lax.dot_general(slab, direction, (((1,), (1,)), ((), ())), precision=high, preferred_element_type=f32)
    update = lax.psum_scatter(part, "col", scatter_dimension=0, tiled=True).T
    row_rms = jnp.sqrt(sum_squares / slab.shape[0])[:, None]
    new_weights = weights - step_rate * update / jnp.maximum(1.0, row_rms)
    return (new_weights, new_first, new_second)


def split(x):
    hi = x.astype(bf16)
    return hi, (x - hi.astype(f32)).astype(bf16)


def start_piece(pieces, r, core, slot, sem):
    half = slot.shape[0] // 2
    for rr, c, first, ref in pieces:
        if rr == r:
            at = pl.multiple_of(lax.rem(core + c, 2) * half + first, 8)
            pltpu.make_async_copy(ref, slot.at[pl.ds(at, ref.shape[0])], sem).start()


def start_block(grads, n, block, col, slot, sem):
    for s in range(1 - n, n):
        if grads[s] is not None:

            @pl.when(col - block == s)
            def _():
                first = 0
                for ref in grads[s]:
                    pltpu.make_async_copy(ref, slot.at[pl.ds(first, ref.shape[0])], sem).start()
                    first += ref.shape[0]


def landed(slot, sem):
    pltpu.make_async_copy(slot, slot, sem).wait()


def nt(a, b):
    return lax.dot_general(a, b, (((1,), (1,)), ((), ())), preferred_element_type=f32)


def by_distance(n, reach, refs):
    out = {s: None for s in range(1 - n, n)}
    out[0] = refs[:1]
    for s in range(1, reach + 1):
        out[s] = refs[2 * s - 1 : 2 * s + 1]
        out[-s] = refs[2 * (reach + s) - 1 : 2 * (reach + s) + 1]
    return out


def product(g, hi, lo):
    g_hi, g_lo = split(g)
    part = jnp.dot(g_hi, hi, preferred_element_type=f32)
    part += jnp.dot(g_hi, lo, preferred_element_type=f32)
    part += jnp.dot(g_lo, hi, preferred_element_type=f32)
    return part


def cut_of(width):
    return (width // 128 + 1) // 2 * 128


def mark_kernel(place, out):
    for k in range(place.shape[0]):
        out[k] = place[k]


def mark(place):
    return pl.pallas_call(
        mark_kernel,
        out_shape=jax.ShapeDtypeStruct(place.shape, place.dtype),
        in_specs=[SM],
        out_specs=SM,
        compiler_params=params(VMEM_MIB),
        cost_estimate=pl.CostEstimate(flops=1024, bytes_accessed=64, transcendentals=0),
    )(place)


def blocked(q_hi, q_lo, d_hi, d_lo):
    return nt(q_hi, d_hi) + nt(q_lo, d_hi) + nt(q_hi, d_lo)


def early_kernel(n, layout, place, *refs):
    count, reach = len(layout), n - 2
    grads = by_distance(n, reach, refs[: 4 * reach + 1])
    refs = refs[4 * reach + 1 :]
    pieces = [(*key, ref) for key, ref in zip(layout, refs[:count])]
    out, s_hi, s_lo, g_all, stage, hi, lo, g_sem, q_sem, out_sem = refs[count:]
    col, pair, core, skip = place[0], place[1], place[2], place[3]
    steps = n - 1

    def fetch(t):
        slot = t % 2
        r = jnp.where(t == 0, skip, jnp.where(t - 1 < skip, t - 1, t))
        if t > 0:
            start_block(grads, n, pair ^ r, col, g_all.at[slot], g_sem.at[slot])
        for k in range(n - 1):

            @pl.when(r == k)
            def _():
                start_piece(pieces, k, core, stage.at[slot], q_sem.at[slot])

    fetch(0)
    fetch(1)
    landed(stage.at[0], q_sem.at[0])
    hi[...], lo[...] = split(stage[0])
    sent = [pltpu.make_async_copy(x, y, out_sem.at[k]) for k, (x, y) in enumerate(((hi, s_hi), (lo, s_lo)))]
    for copy in sent:
        copy.start()
    for t in range(1, steps):
        slot = t % 2
        if t + 1 < steps:
            fetch(t + 1)
        landed(stage.at[slot], q_sem.at[slot])
        landed(g_all.at[slot], g_sem.at[slot])
        part = product(g_all[slot], *split(stage[slot]))
        if t == 1:
            out[...] = part
        else:
            out[...] += part
    for copy in sent:
        copy.wait()


def middle_kernel(n, place, *refs):
    reach = n - 1
    grads = by_distance(n, reach, refs[: 4 * reach + 1])
    acc, s_hi, s_lo, out, r_hi, r_lo, g_all, held, q_hi, q_lo, g_sem, q_sem, out_sem = refs[4 * reach + 1 :]
    col, pair, skip = place[0], place[1], place[3]
    brought = [pltpu.make_async_copy(x, y, q_sem.at[k]) for k, (x, y) in enumerate(((s_hi, q_hi), (s_lo, q_lo), (acc, held)))]
    start_block(grads, n, pair ^ skip, col, g_all.at[0], g_sem.at[0])
    for copy in brought:
        copy.start()
    start_block(grads, n, pair ^ (n - 1), col, g_all.at[1], g_sem.at[1])
    landed(g_all.at[0], g_sem.at[0])
    g_hi, g_lo = split(g_all[0])
    brought[0].wait()
    part = jnp.dot(g_hi, q_hi[...], preferred_element_type=f32)
    part += jnp.dot(g_lo, q_hi[...], preferred_element_type=f32)
    brought[1].wait()
    part += jnp.dot(g_hi, q_lo[...], preferred_element_type=f32)
    brought[2].wait()
    held[...] += part
    sent = pltpu.make_async_copy(held, out, out_sem)
    sent.start()
    landed(g_all.at[1], g_sem.at[1])
    r_hi[...], r_lo[...] = split(g_all[1])
    sent.wait()


def rotate_kernel(n, layout, place, *refs):
    count = len(layout)
    pieces = [(*key, ref) for key, ref in zip(layout, refs[:count])]
    given, refs = refs[count : count + 7], refs[count + 7 :]
    made, refs = refs[:5], refs[5:]
    held, refs = refs[:7], refs[7:]
    acc, g_hi, g_lo, first, second, s_hi, s_lo = held
    results, (stage, q_hi, q_lo, p_sem, in_sem, out_sem) = refs[:5], refs[5:]
    nf, ns, d, top, bottom = results
    core, lead = place[2], place[4]
    half, last = stage.shape[1], n - 1
    for _, c, start, ref in pieces:
        pltpu.make_async_copy(ref, stage.at[c, pl.ds(start, ref.shape[0])], p_sem.at[c]).start()
    brought = [pltpu.make_async_copy(x, y, in_sem.at[k]) for k, (x, y) in enumerate(zip(given, held))]
    for copy in brought[1:3]:
        copy.start()
    for c in range(2):
        landed(stage.at[c], p_sem.at[c])
        if c:
            for k in (0, 3, 4):
                brought[k].start()

            @pl.when(lead != last)
            def _():
                brought[5].start()
                brought[6].start()

        at = pl.multiple_of(lax.rem(core + c, 2) * half, 16)
        q_hi[pl.ds(at, half)], q_lo[pl.ds(at, half)] = split(stage[c])
    for copy in brought[1:3]:
        copy.wait()
    total = jnp.dot(g_hi[...], q_hi[...], preferred_element_type=f32)
    total += jnp.dot(g_hi[...], q_lo[...], preferred_element_type=f32)
    total += jnp.dot(g_lo[...], q_hi[...], preferred_element_type=f32)
    for k in (0, 3, 4):
        brought[k].wait()
    total += acc[...]
    nf[...] = 0.9 * first[...] + 0.1 * total
    ns[...] = 0.999 * second[...] + 0.001 * total * total
    d[...] = nf[...] / bias_first / (jnp.sqrt(ns[...] / bias_second) + epsilon)
    sent = [pltpu.make_async_copy(x, y, out_sem.at[k]) for k, (x, y) in enumerate(zip(results, made))]
    for copy in sent[:3]:
        copy.start()
    d_hi, d_lo = split(d[...])
    cut = top.shape[0] - 8
    ones = jnp.ones((8, d.shape[1]), bf16)
    hi, rest = split(d[...] * d[...])
    top[cut:] = nt(ones, hi) + nt(ones, rest)

    def put(a, b):
        u = blocked(a[...], b[...], d_hi, d_lo)
        top[:cut] = u[:cut]
        bottom[...] = u[cut:]

    @pl.when(lead == last)
    def _():
        put(q_hi, q_lo)

    @pl.when(lead != last)
    def _():
        brought[5].wait()
        brought[6].wait()
        put(s_hi, s_lo)

    sent[3].start()
    sent[4].start()
    for copy in sent:
        copy.wait()


ANY = pl.BlockSpec(memory_space=pl.ANY)
VM = pl.BlockSpec(memory_space=pltpu.VMEM)
SM = pl.BlockSpec(memory_space=pltpu.SMEM)


VMEM_MIB = 44


def params(mib):
    return pltpu.CompilerParams(vmem_limit_bytes=mib * 2**20)


def cost(products, rows, width):
    return pl.CostEstimate(flops=int(6 * products * rows * width * width), bytes_accessed=8 * width * width, transcendentals=0)


def early(place, grads, keys, pieces, n):
    rows, width = grads[0].shape
    shape = jax.ShapeDtypeStruct
    return pl.pallas_call(
        lambda *refs: early_kernel(n, keys, *refs),
        out_shape=[shape((rows, width), f32)] + [shape((width, width), bf16)] * 2,
        in_specs=[SM] + [ANY] * (len(grads) + len(pieces)),
        out_specs=[VM, ANY, ANY],
        scratch_shapes=[
            pltpu.VMEM((2, rows, width), f32),
            pltpu.VMEM((2, width, width), f32),
            pltpu.VMEM((width, width), bf16),
            pltpu.VMEM((width, width), bf16),
        ]
        + [pltpu.SemaphoreType.DMA((2,))] * 3,
        compiler_params=params(VMEM_MIB),
        cost_estimate=cost(n - 2, rows, width),
        name="early",
    )(place, *grads, *pieces)


def middle(place, grads, acc, s_hi, s_lo, n):
    rows, width = acc.shape
    shape = jax.ShapeDtypeStruct
    return pl.pallas_call(
        lambda *refs: middle_kernel(n, *refs),
        out_shape=[shape((rows, width), f32)] + [shape((rows, width), bf16)] * 2,
        in_specs=[SM] + [ANY] * (len(grads) + 3),
        out_specs=[ANY] + [VM] * 2,
        scratch_shapes=[pltpu.VMEM((2, rows, width), f32), pltpu.VMEM((rows, width), f32)]
        + [pltpu.VMEM((width, width), bf16)] * 2
        + [pltpu.SemaphoreType.DMA((2,)), pltpu.SemaphoreType.DMA((3,)), pltpu.SemaphoreType.DMA],
        compiler_params=params(VMEM_MIB),
        cost_estimate=cost(1, rows, width),
        name="middle",
    )(place, *grads, acc, s_hi, s_lo)


def rotate(place, keys, pieces, given, n):
    rows, width = given[0].shape
    half, cut = width // 2, cut_of(width)
    shape = jax.ShapeDtypeStruct
    return pl.pallas_call(
        lambda *refs: rotate_kernel(n, keys, *refs),
        out_shape=[shape((rows, width), f32)] * 3 + [shape((cut + 8, rows), f32), shape((width - cut, rows), f32)],
        in_specs=[SM] + [ANY] * (len(pieces) + len(given)),
        out_specs=[ANY] * 5,
        scratch_shapes=[pltpu.VMEM(x.shape, x.dtype) for x in given]
        + [pltpu.VMEM((rows, width), f32)] * 3
        + [pltpu.VMEM((cut + 8, rows), f32), pltpu.VMEM((width - cut, rows), f32)]
        + [pltpu.VMEM((2, half, width), f32)]
        + [pltpu.VMEM((width, width), bf16)] * 2
        + [pltpu.SemaphoreType.DMA((k,)) for k in (2, len(given), 5)],
        compiler_params=params(VMEM_MIB),
        cost_estimate=cost(2, rows, width),
        name="rotate",
    )(place, *pieces, *given)


def back_kernel(n, layout, place, *refs):
    count = len(layout)
    direction, top, bottom = refs[0:3]
    pieces = [(*key, ref) for key, ref in zip(layout, refs[3 : 3 + count])]
    outs, (stage, u, q_sem) = refs[3 + count : -3], refs[-3:]
    col, pair, core, lead = place[0], place[1], place[2], place[4]
    for r in range(min(2, n)):
        start_piece(pieces, r, core, stage.at[r % 2], q_sem.at[r % 2])
    hi, lo = split(direction[...])
    cut = top.shape[0] - 8

    @pl.loop(0, n)
    def _(r):
        slot = lax.rem(r, 2)
        landed(stage.at[slot], q_sem.at[slot])
        block = pair ^ r
        step = jnp.where(block > col, n - 1 - block + col, block + n - 1 - col)
        spot = jnp.where(block == col, 2 * n - 4, jnp.where(block > col, step - 1, n - 3 + step))

        @pl.when(r != lead)
        def _():
            u[...] = blocked(*split(stage[slot]), hi, lo)

        @pl.when(r == lead)
        def _():
            u[:cut] = top[:cut]
            u[cut:] = bottom[...]

        for k in range(2, n):

            @pl.when(r + 2 == k)
            def _():
                start_piece(pieces, k, core, stage.at[k % 2], q_sem.at[k % 2])

        for k in range(2 * n - 3):

            @pl.when((spot == k) & ((block == col) | (step > 0)))
            def _():
                outs[2 * k][:cut] = u[:cut]
                outs[2 * k][cut:] = top[cut:]
                outs[2 * k + 1][...] = u[cut:]


def back(place, direction, top, bottom, keys, pieces, n):
    rows, width = direction.shape
    cut = cut_of(width)
    shapes = [jax.ShapeDtypeStruct((cut + 8, rows), f32), jax.ShapeDtypeStruct((width - cut, rows), f32)]
    return pl.pallas_call(
        lambda *refs: back_kernel(n, keys, *refs),
        out_shape=shapes * (2 * n - 3),
        in_specs=[SM] + [VM] * 3 + [ANY] * len(pieces),
        out_specs=[VM] * (4 * n - 6),
        scratch_shapes=[pltpu.VMEM((2, width, width), f32), pltpu.VMEM((width, rows), f32), pltpu.SemaphoreType.DMA((2,))],
        compiler_params=params(VMEM_MIB),
        cost_estimate=pl.CostEstimate(flops=6 * rows * width * width * (n - 1), bytes_accessed=4 * n * width * width, transcendentals=0),
        name="back",
    )(place, direction, top, bottom, *pieces)


def finish_top_kernel(deep, weights, a0, a1, a2, out, norm, held, sem):
    cut = held.shape[1]
    total = a0[...] + a1[...] + a2[...]
    norm[...] = jnp.maximum(1.0, jnp.sqrt(total[cut:] / deep))
    held[...] = weights[:, :cut] - (step_rate * total[:cut] / norm[:1]).T
    copy = pltpu.make_async_copy(held, out.at[:, pl.ds(0, cut)], sem)
    copy.start()
    copy.wait()


def finish_bottom_kernel(weights, norm, b0, b1, b2, _, out, held, sem):
    cut = weights.shape[1] - held.shape[1]
    total = b0[...] + b1[...] + b2[...]
    held[...] = weights[:, cut:] - (step_rate * total / norm[:1]).T
    copy = pltpu.make_async_copy(held, out.at[:, pl.ds(cut, held.shape[1])], sem)
    copy.start()
    copy.wait()


def finish(weights, parts, deep):
    rows, width = weights.shape
    cut = cut_of(width)
    shape = jax.ShapeDtypeStruct(weights.shape, f32)
    some, norm = pl.pallas_call(
        lambda *refs: finish_top_kernel(deep, *refs),
        out_shape=[shape, jax.ShapeDtypeStruct((8, rows), f32)],
        in_specs=[VM] * 4,
        out_specs=[ANY, VM],
        scratch_shapes=[pltpu.VMEM((rows, cut), f32), pltpu.SemaphoreType.DMA],
        compiler_params=params(VMEM_MIB),
        cost_estimate=cost(0.1, rows, width),
        name="finish_top",
    )(weights, *parts[:3])
    return pl.pallas_call(
        finish_bottom_kernel,
        out_shape=shape,
        in_specs=[VM] * 5 + [ANY],
        out_specs=ANY,
        scratch_shapes=[pltpu.VMEM((rows, width - cut), f32), pltpu.SemaphoreType.DMA],
        input_output_aliases={5: 0},
        compiler_params=params(VMEM_MIB),
        cost_estimate=cost(0.1, rows, width),
        name="finish_bottom",
    )(weights, norm, *parts[3:], some)


def swapped(n_row, bit):
    return [(i, i ^ bit) for i in range(n_row)]


def gather_basis(q, n_row):
    bits = []
    bit = 2
    while bit < n_row:
        bits.append(bit)
        bit *= 2
    half = q.shape[0] // 2
    keys, arrays = [], []

    def put(r, start, x):
        keys.append((r, 0, start))
        arrays.append(x)
        keys.append((r, 1, start))
        arrays.append(lax.ppermute(x, "row", swapped(n_row, 1)))

    put(0, 0, q)
    for start, order, x in ((0, bits, q[:half]), (half, bits[::-1], q[half:])):
        held = [(0, x)]
        for b in order:
            fresh = [(r | (b // 2), lax.ppermute(v, "row", swapped(n_row, b))) for r, v in held]
            for r, v in fresh:
                put(r, start, v)
            held += fresh
    return keys, arrays


def gather_line(g, n):
    rights, lefts = [], []
    half = g.shape[0] // 2
    a = b = [g[:half], g[half:]]
    for s in range(1, n):
        right = [(i, i + 1) for i in range(s - 1, n - 1)]
        left = [(i, i - 1) for i in range(n - s, 0, -1)]
        a = [lax.ppermute(x, "col", right) for x in a]
        b = [lax.ppermute(x, "col", left) for x in b]
        rights += a
        lefts += b
    return rights, lefts


def scatter_line(parts, blocks, n):
    got = [[None, None] for _ in parts]
    for s in range(n - 1):
        for h, part in enumerate(parts):
            for way in (0, 1):
                load = part if s == 0 else blocks[2 * (way * (n - 2) + s - 1) + h] + got[h][way]
                perm = [(i, i + 1) for i in range(s + 1)] if way == 0 else [(i, i - 1) for i in range(n - 1 - s, n)]
                got[h][way] = lax.ppermute(load, "col", perm)
    return [x for h in range(len(parts)) for x in (blocks[2 * (2 * n - 4) + h], *got[h])]


def solution(mesh):
    n_row, n_col = mesh.shape["row"], mesh.shape["col"]
    pairs = n_row // 2
    meets = n_row == 2 * n_col and pairs & (pairs - 1) == 0 and n_col > 2

    def per_device(gradient, first_moment, second_moment, weights, eigenbasis):
        width, n = gradient.shape[1], n_col
        if not (meets and width % 128 == 0 and eigenbasis.shape[0] % 32 == 0 and gradient.shape[0] % 16 == 0):
            return plain(gradient, first_moment, second_moment, weights, eigenbasis)
        row, col = lax.axis_index("row"), lax.axis_index("col")
        pair = row // 2
        end = (col == 0) | (col == n - 1)
        lead = jnp.where(end, pair ^ (n - 1 - col), n - 1)
        skip = jnp.where(lead == n - 1, 0, lead)
        place = jnp.stack([col, pair, row % 2, skip, lead]).astype(jnp.int32)
        keys, pieces = gather_basis(eigenbasis, n_row)
        rights, lefts = gather_line(gradient, n)
        place = mark(place)

        def some(wanted):
            return [key for key in keys if wanted(key)], [x for key, x in zip(keys, pieces) if wanted(key)]

        acc, s_hi, s_lo = early(place, [gradient, *rights[: 2 * n - 4], *lefts[: 2 * n - 4]], *some(lambda key: key[0] < n - 1), n)
        acc, g_hi, g_lo = middle(place, [gradient, *rights, *lefts], acc, s_hi, s_lo, n)
        given = [acc, g_hi, g_lo, first_moment, second_moment, s_hi, s_lo]
        new_first, new_second, direction, top, bottom = rotate(place, *some(lambda key: key[0] == n - 1), given, n)
        blocks = back(place, direction, top, bottom, keys, pieces, n)
        new_weights = finish(weights, scatter_line([top, bottom], blocks, n), width * n)
        return (new_weights, new_first, new_second)

    spec = P("row", "col")
    return jax.shard_map(per_device, mesh=mesh, in_specs=(spec,) * 5, out_specs=(spec,) * 3, check_vma=False)
```

profile of v0, /device:TPU:20, one launch (start us, length us, event | category | flops | bytes accessed | tf_op | source)
XLA Modules:
  0.0 262.2 jit_solution(17818879641144655239)
XLA Ops:
  10.5 3.5 %collective-permute-start.7 = (f32[128,1152]{1,0:T(8,128)S(1)}, f32[128,1152]{1,0:T(8,128)S(1)}, u32[]{:S(2)}, u32[]{:S(2)}) collective-permute-start(f32[128,1152]{1,0:T(8,128)S(1)} %get-tuple-element.51), channel_id=1, source_target_pairs={{0,1},{1,2},{2,3},{4,5},{5,6},{6,7},{8,9},{9,10},{10,11},{12,13},{... | collective-permute-start | bytes 1769480 | tf_op jit(solution)/shard_map/ppermute | solution.py:463
  14.0 6.0 %collective-permute-done.12.refs_6_.refs_8_ = f32[128,1152]{1,0:T(8,128)S(1)} collective-permute-done((f32[128,1152]{1,0:T(8,128)S(1)}, f32[128,1152]{1,0:T(8,128)S(1)}, u32[]{:S(2)}, u32[]{:S(2)}) %collective-permute-start.12) | collective-permute-done | bytes 589856 | tf_op jit(solution)/shard_map/ppermute | solution.py:464
  26.7 4.8 %collective-permute-done.13.refs_7_.refs_9_ = f32[128,1152]{1,0:T(8,128)S(1)} collective-permute-done((f32[128,1152]{1,0:T(8,128)S(1)}, f32[128,1152]{1,0:T(8,128)S(1)}, u32[]{:S(2)}, u32[]{:S(2)}) %collective-permute-start.13) | collective-permute-done | bytes 589856 | tf_op jit(solution)/shard_map/ppermute | solution.py:464
  32.1 4.4 %collective-permute-start.15 = (f32[128,1152]{1,0:T(8,128)S(1)}, f32[128,1152]{1,0:T(8,128)}, u32[]{:S(2)}, u32[]{:S(2)}) collective-permute-start(f32[128,1152]{1,0:T(8,128)S(1)} %collective-permute-done.13.refs_7_.refs_9_), channel_id=1, source_target_pairs={{2,1},{1,0},{6,5},{5,4},{10,9},{9,8},{14,13},{13,12},{18,17},{17,1... | collective-permute-start | bytes 1769480 | tf_op jit(solution)/shard_map/ppermute | solution.py:464
  43.8 11.0 %collective-permute-done.15.refs_9_.refs_11_ = f32[128,1152]{1,0:T(8,128)} collective-permute-done((f32[128,1152]{1,0:T(8,128)S(1)}, f32[128,1152]{1,0:T(8,128)}, u32[]{:S(2)}, u32[]{:S(2)}) %collective-permute-start.15) | collective-permute-done | bytes 589856 | tf_op jit(solution)/shard_map/ppermute | solution.py:464
  59.0 4.5 %collective-permute-done.3.refs_16_.refs_12_ = f32[288,1152]{1,0:T(8,128)S(1)} collective-permute-done((f32[288,1152]{1,0:T(8,128)S(1)}, f32[288,1152]{1,0:T(8,128)S(1)}, u32[]{:S(2)}, u32[]{:S(2)}) %collective-permute-start.3) | collective-permute-done | bytes 1327136 | tf_op jit(solution)/shard_map/ppermute | solution.py:449
  63.6 7.7 %collective-permute-done.9.refs_5_ = f32[128,1152]{1,0:T(8,128)} collective-permute-done((f32[128,1152]{1,0:T(8,128)S(1)}, f32[128,1152]{1,0:T(8,128)}, u32[]{:S(2)}, u32[]{:S(2)}) %collective-permute-start.9) | collective-permute-done | bytes 589856 | tf_op jit(solution)/shard_map/ppermute | solution.py:463
  71.2 18.8 %collective-permute-done.20.refs_14_.refs_8_ = f32[288,1152]{1,0:T(8,128)S(1)} collective-permute-done((f32[288,1152]{1,0:T(8,128)S(1)}, f32[288,1152]{1,0:T(8,128)S(1)}, u32[]{:S(2)}, u32[]{:S(2)}) %collective-permute-start.20) | collective-permute-done | bytes 1327136 | tf_op jit(solution)/shard_map/ppermute | solution.py:449
  93.9 8.5 %collective-permute-done.10.refs_6_ = f32[128,1152]{1,0:T(8,128)S(1)} collective-permute-done((f32[128,1152]{1,0:T(8,128)S(1)}, f32[128,1152]{1,0:T(8,128)S(1)}, u32[]{:S(2)}, u32[]{:S(2)}) %collective-permute-start.10) | collective-permute-done | bytes 589856 | tf_op jit(solution)/shard_map/ppermute | solution.py:463
  106.3 15.0 %collective-permute-done.1.refs_1_.refs_10_ = f32[288,1152]{1,0:T(8,128)S(1)} collective-permute-done((f32[288,1152]{1,0:T(8,128)S(1)}, f32[288,1152]{1,0:T(8,128)S(1)}, u32[]{:S(2)}, u32[]{:S(2)}) %collective-permute-start.1) | collective-permute-done | bytes 1327136 | tf_op jit(solution)/shard_map/ppermute | solution.py:449
  121.3 10.5 %collective-permute-done.4.refs_3_.refs_16_ = f32[288,1152]{1,0:T(8,128)} collective-permute-done((f32[288,1152]{1,0:T(8,128)S(1)}, f32[288,1152]{1,0:T(8,128)}, u32[]{:S(2)}, u32[]{:S(2)}) %collective-permute-start.4) | collective-permute-done | bytes 1327136 | tf_op jit(solution)/shard_map/ppermute | solution.py:449
  131.8 5.2 %collective-permute-start.11 = (f32[128,1152]{1,0:T(8,128)}, f32[128,1152]{1,0:T(8,128)}, u32[]{:S(2)}, u32[]{:S(2)}) collective-permute-start(f32[128,1152]{1,0:T(8,128)} %collective-permute-done.9.refs_5_), channel_id=1, source_target_pairs={{2,3},{6,7},{10,11},{14,15},{18,19},{22,23},{26,27},{30,31}} | collective-permute-start | bytes 1769480 | tf_op jit(solution)/shard_map/ppermute | solution.py:463
  149.7 10.9 %early.1 = (f32[256,1152]{1,0:T(8,128)S(1)}, bf16[1152,1152]{1,0:T(8,128)(2,1)}, bf16[1152,1152]{1,0:T(8,128)(2,1)}) custom-call(s32[5]{0:T(128)S(1)} %shard_map.76.refs_0_, f32[256,1152]{1,0:T(8,128)S(1)} %copy-done, f32[128,1152]{1,0:T(8,128)S(1)} %copy-done.9, f32[128,1152]{1,0:T(8,128)S(1)} %copy-done.15, f32[128,1152]{1,0:T(8,128)S(1)} %copy-done.17, ...), custom_call_target="tpu_custom_call" | custom-call | flops 4076863488 | bytes 10616832 | tf_op jit(solution)/shard_map/early/pallas_call | solution.py:265
  161.7 6.3 %middle.1 = (f32[256,1152]{1,0:T(8,128)S(1)}, bf16[256,1152]{1,0:T(8,128)(2,1)S(1)}, bf16[256,1152]{1,0:T(8,128)(2,1)S(1)}) custom-call(s32[5]{0:T(128)S(1)} %shard_map.76.refs_0_, f32[256,1152]{1,0:T(8,128)} %refs_1_.3, f32[128,1152]{1,0:T(8,128)S(1)} %copy-done.10, f32[128,1152]{1,0:T(8,128)S(1)} %copy-done.15, f32[128,1152]{1,0:T(8,128)S(1)} %copy-done.17, ...), custom_call_target="tpu_custom_call" | custom-call | flops 2038431744 | bytes 10616832 | tf_op jit(solution)/shard_map/middle/pallas_call | solution.py:286
  168.1 11.9 %rotate.1 = (f32[256,1152]{1,0:T(8,128)}, f32[256,1152]{1,0:T(8,128)}, f32[256,1152]{1,0:T(8,128)S(1)}, f32[648,256]{1,0:T(8,128)S(1)}, f32[512,256]{1,0:T(8,128)S(1)}) custom-call(s32[5]{0:T(128)S(1)} %shard_map.76.refs_0_, f32[288,1152]{1,0:T(8,128)S(1)} %collective-permute-done.1.refs_1_.refs_10_, f32[288,1152]{1,0:T(8,128)} %collective-permute-done.2.refs_2_.refs_11_, ...), custom_call_target="tpu_custom_call" | custom-call | flops 4076863488 | bytes 10616832 | tf_op jit(solution)/shard_map/rotate/pallas_call | solution.py:304
  184.2 11.2 %back.1 = (f32[648,256]{1,0:T(8,128)S(1)}, f32[512,256]{1,0:T(8,128)S(1)}, f32[648,256]{1,0:T(8,128)S(1)}, f32[512,256]{1,0:T(8,128)S(1)}, f32[648,256]{1,0:T(8,...) custom-call(s32[5]{0:T(128)S(1)} %shard_map.76.refs_0_, ...), custom_call_target="tpu_custom_call" | custom-call | flops 6115295232 | bytes 21233664 | tf_op jit(solution)/shard_map/back/pallas_call | solution.py:368
  195.3 4.3 %collective-permute-done.28 = f32[648,256]{1,0:T(8,128)S(1)} collective-permute-done((f32[648,256]{1,0:T(8,128)S(1)}, f32[648,256]{1,0:T(8,128)S(1)}, u32[]{:S(2)}, u32[]{:S(2)}) %collective-permute-start.28) | collective-permute-done | bytes 663584 | tf_op jit(solution)/shard_map/ppermute | solution.py:477
  203.0 7.8 %collective-permute-done.34 = f32[512,256]{1,0:T(8,128)S(1)} collective-permute-done((f32[512,256]{1,0:T(8,128)S(1)}, f32[512,256]{1,0:T(8,128)S(1)}, u32[]{:S(2)}, u32[]{:S(2)}) %collective-permute-start.34) | collective-permute-done | bytes 524320 | tf_op jit(solution)/shard_map/ppermute | solution.py:477
  214.2 10.8 %collective-permute-done.29 = f32[648,256]{1,0:T(8,128)S(1)} collective-permute-done((f32[648,256]{1,0:T(8,128)S(1)}, f32[648,256]{1,0:T(8,128)S(1)}, u32[]{:S(2)}, u32[]{:S(2)}) %collective-permute-start.29) | collective-permute-done | bytes 663584 | tf_op jit(solution)/shard_map/ppermute | solution.py:477
  227.2 4.0 %collective-permute-start.27 = (f32[648,256]{1,0:T(8,128)S(1)}, f32[648,256]{1,0:T(8,128)S(1)}, u32[]{:S(2)}, u32[]{:S(2)}) collective-permute-start(f32[648,256]{1,0:T(8,128)S(1)} %add.31), channel_id=1, source_target_pairs={{0,1},{1,2},{2,3},{4,5},{5,6},{6,7},{8,9},{9,10},{10,11},{12,13},{... | collective-permute-start | bytes 1990664 | tf_op jit(solution)/shard_map/ppermute | solution.py:477
  231.1 5.1 %collective-permute-done.35 = f32[512,256]{1,0:T(8,128)S(1)} collective-permute-done((f32[512,256]{1,0:T(8,128)S(1)}, f32[512,256]{1,0:T(8,128)S(1)}, u32[]{:S(2)}, u32[]{:S(2)}) %collective-permute-start.35) | collective-permute-done | bytes 524320 | tf_op jit(solution)/shard_map/ppermute | solution.py:477
  238.5 4.0 %collective-permute-start.33 = (f32[512,256]{1,0:T(8,128)S(1)}, f32[512,256]{1,0:T(8,128)S(1)}, u32[]{:S(2)}, u32[]{:S(2)}) collective-permute-start(f32[512,256]{1,0:T(8,128)S(1)} %add.35), channel_id=1, source_target_pairs={{0,1},{1,2},{2,3},{4,5},{5,6},{6,7},{8,9},{9,10},{10,11},{12,13},{... | collective-permute-start | bytes 1572872 | tf_op jit(solution)/shard_map/ppermute | solution.py:477
  242.5 8.0 %collective-permute-done.30.refs_3_ = f32[648,256]{1,0:T(8,128)S(1)} collective-permute-done((f32[648,256]{1,0:T(8,128)S(1)}, f32[648,256]{1,0:T(8,128)S(1)}, u32[]{:S(2)}, u32[]{:S(2)}) %collective-permute-start.30) | collective-permute-done | bytes 663584 | tf_op jit(solution)/shard_map/ppermute | solution.py:477
  251.7 9.3 %collective-permute-done.36.b2 = f32[512,256]{1,0:T(8,128)S(1)} collective-permute-done((f32[512,256]{1,0:T(8,128)S(1)}, f32[512,256]{1,0:T(8,128)S(1)}, u32[]{:S(2)}, u32[]{:S(2)}) %collective-permute-start.36) | collective-permute-done | bytes 524320 | tf_op jit(solution)/shard_map/ppermute | solution.py:477
  (130 shorter events, 67.4 us)
Async XLA Ops:
  4.3 27.7 %collective-permute-start.6 = (f32[128,1152]{1,0:T(8,128)S(1)}, f32[128,1152]{1,0:T(8,128)S(1)}, u32[]{:S(2)}, u32[]{:S(2)}) collective-permute-start(f32[128,1152]{1,0:T(8,128)S(1)} %get-tuple-element.52), channel_id=1, source_target_pairs={{0,1},{1,2},{2,3},{4,5},{5,6},{6,7},{8,9},{9,10},{10,11},{12,13},{... | collective-permute-start | bytes 1769480 | tf_op jit(solution)/shard_map/ppermute | solution.py:463
  10.5 26.8 %collective-permute-start.7 = (f32[128,1152]{1,0:T(8,128)S(1)}, f32[128,1152]{1,0:T(8,128)S(1)}, u32[]{:S(2)}, u32[]{:S(2)}) collective-permute-start(f32[128,1152]{1,0:T(8,128)S(1)} %get-tuple-element.51), channel_id=1, source_target_pairs={{0,1},{1,2},{2,3},{4,5},{5,6},{6,7},{8,9},{9,10},{10,11},{12,13},{... | collective-permute-start | bytes 1769480 | tf_op jit(solution)/shard_map/ppermute | solution.py:463
  25.2 33.9 %collective-permute-start = (f32[288,1152]{1,0:T(8,128)S(1)}, f32[288,1152]{1,0:T(8,128)S(1)}, u32[]{:S(2)}, u32[]{:S(2)}) collective-permute-start(f32[288,1152]{1,0:T(8,128)S(1)} %get-tuple-element.50), channel_id=1, source_target_pairs={{0,8},{4,12},{8,0},{12,4},{16,24},{20,28},{24,16},{28,20},{1,9},{5... | collective-permute-start | bytes 3981320 | tf_op jit(solution)/shard_map/ppermute | solution.py:449
  31.6 32.0 %collective-permute-start.3 = (f32[288,1152]{1,0:T(8,128)S(1)}, f32[288,1152]{1,0:T(8,128)S(1)}, u32[]{:S(2)}, u32[]{:S(2)}) collective-permute-start(f32[288,1152]{1,0:T(8,128)S(1)} %get-tuple-element.49), channel_id=1, source_target_pairs={{0,16},{4,20},{8,24},{12,28},{16,0},{20,4},{24,8},{28,12},{1,17},{... | collective-permute-start | bytes 3981320 | tf_op jit(solution)/shard_map/ppermute | solution.py:449
  43.3 46.7 %collective-permute-start.20 = (f32[288,1152]{1,0:T(8,128)S(1)}, f32[288,1152]{1,0:T(8,128)S(1)}, u32[]{:S(2)}, u32[]{:S(2)}) collective-permute-start(f32[288,1152]{1,0:T(8,128)S(1)} %get-tuple-element.50), channel_id=1, source_target_pairs={{0,16},{4,20},{8,24},{12,28},{16,0},{20,4},{24,8},{28,12},{1,17},{... | collective-permute-start | bytes 3981320 | tf_op jit(solution)/shard_map/ppermute | solution.py:449
  57.5 34.8 %collective-permute-start.23 = (f32[288,1152]{1,0:T(8,128)S(1)}, f32[288,1152]{1,0:T(8,128)S(1)}, u32[]{:S(2)}, u32[]{:S(2)}) collective-permute-start(f32[288,1152]{1,0:T(8,128)S(1)} %get-tuple-element.49), channel_id=1, source_target_pairs={{0,8},{4,12},{8,0},{12,4},{16,24},{20,28},{24,16},{28,20},{1,9},{5... | collective-permute-start | bytes 3981320 | tf_op jit(solution)/shard_map/ppermute | solution.py:449
  59.0 45.7 %collective-permute-start.19 = (f32[288,1152]{1,0:T(8,128)S(1)}, f32[288,1152]{1,0:T(8,128)S(1)}, u32[]{:S(2)}, u32[]{:S(2)}) collective-permute-start(f32[288,1152]{1,0:T(8,128)S(1)} %collective-permute-done.refs_12_.refs_6_), channel_id=1, source_target_pairs={{0,4},{4,0},{8,12},{12,8},{16,20},{20,16},{24,28},{28,24},{1,5},{5... | collective-permute-start | bytes 3981320 | tf_op jit(solution)/shard_map/ppermute | solution.py:443
  63.6 42.3 %collective-permute-start.22 = (f32[288,1152]{1,0:T(8,128)S(1)}, f32[288,1152]{1,0:T(8,128)S(1)}, u32[]{:S(2)}, u32[]{:S(2)}) collective-permute-start(f32[288,1152]{1,0:T(8,128)S(1)} %collective-permute-done.3.refs_16_.refs_12_), channel_id=1, source_target_pairs={{0,4},{4,0},{8,12},{12,8},{16,20},{20,16},{24,28},{28,24},{1,5},{5... | collective-permute-start | bytes 3981320 | tf_op jit(solution)/shard_map/ppermute | solution.py:443
  71.2 67.3 %collective-permute-start.18 = (f32[576,1152]{1,0:T(8,128)S(1)}, f32[576,1152]{1,0:T(8,128)S(1)}, u32[]{:S(2)}, u32[]{:S(2)}) collective-permute-start(f32[576,1152]{1,0:T(8,128)S(1)} %copy-done.23), channel_id=1, source_target_pairs={{0,4},{4,0},{8,12},{12,8},{16,20},{20,16},{24,28},{28,24},{1,5},{5... | collective-permute-start | bytes 7962632 | tf_op jit(solution)/shard_map/ppermute | solution.py:443
  92.3 29.0 %collective-permute-start.1 = (f32[288,1152]{1,0:T(8,128)S(1)}, f32[288,1152]{1,0:T(8,128)S(1)}, u32[]{:S(2)}, u32[]{:S(2)}) collective-permute-start(f32[288,1152]{1,0:T(8,128)S(1)} %collective-permute-done.refs_12_.refs_6_), channel_id=1, source_target_pairs={{0,16},{4,20},{8,24},{12,28},{16,0},{20,4},{24,8},{28,12},{1,17},{... | collective-permute-start | bytes 3981320 | tf_op jit(solution)/shard_map/ppermute | solution.py:449
  103.3 28.5 %collective-permute-start.4 = (f32[288,1152]{1,0:T(8,128)S(1)}, f32[288,1152]{1,0:T(8,128)}, u32[]{:S(2)}, u32[]{:S(2)}) collective-permute-start(f32[288,1152]{1,0:T(8,128)S(1)} %collective-permute-done.3.refs_16_.refs_12_), channel_id=1, source_target_pairs={{0,8},{4,12},{8,0},{12,4},{16,24},{20,28},{24,16},{28,20},{1,9},{5... | collective-permute-start | bytes 3981320 | tf_op jit(solution)/shard_map/ppermute | solution.py:449
  105.8 26.0 %collective-permute-start.21 = (f32[288,1152]{1,0:T(8,128)S(1)}, f32[288,1152]{1,0:T(8,128)S(1)}, u32[]{:S(2)}, u32[]{:S(2)}) collective-permute-start(f32[288,1152]{1,0:T(8,128)S(1)} %collective-permute-done.20.refs_14_.refs_8_), channel_id=1, source_target_pairs={{0,4},{4,0},{8,12},{12,8},{16,20},{20,16},{24,28},{28,24},{1,5},{5... | collective-permute-start | bytes 3981320 | tf_op jit(solution)/shard_map/ppermute | solution.py:443
  105.8 31.2 %collective-permute-start.24 = (f32[288,1152]{1,0:T(8,128)S(1)}, f32[288,1152]{1,0:T(8,128)S(1)}, u32[]{:S(2)}, u32[]{:S(2)}) collective-permute-start(f32[288,1152]{1,0:T(8,128)S(1)} %collective-permute-done.23.refs_18_.refs_14_), channel_id=1, source_target_pairs={{0,4},{4,0},{8,12},{12,8},{16,20},{20,16},{24,28},{28,24},{1,5},{5... | collective-permute-start | bytes 3981320 | tf_op jit(solution)/shard_map/ppermute | solution.py:443
  121.3 46.7 %collective-permute-start.2 = (f32[288,1152]{1,0:T(8,128)S(1)}, f32[288,1152]{1,0:T(8,128)}, u32[]{:S(2)}, u32[]{:S(2)}) collective-permute-start(f32[288,1152]{1,0:T(8,128)S(1)} %collective-permute-done.1.refs_1_.refs_10_), channel_id=1, source_target_pairs={{0,4},{4,0},{8,12},{12,8},{16,20},{20,16},{24,28},{28,24},{1,5},{5... | collective-permute-start | bytes 3981320 | tf_op jit(solution)/shard_map/ppermute | solution.py:443
  131.8 36.2 %collective-permute-start.5 = (f32[288,1152]{1,0:T(8,128)}, f32[288,1152]{1,0:T(8,128)}, u32[]{:S(2)}, u32[]{:S(2)}) collective-permute-start(f32[288,1152]{1,0:T(8,128)} %collective-permute-done.4.refs_3_.refs_16_), channel_id=1, source_target_pairs={{0,4},{4,0},{8,12},{12,8},{16,20},{20,16},{24,28},{28,24},{1,5},{5... | collective-permute-start | bytes 3981320 | tf_op jit(solution)/shard_map/ppermute | solution.py:443
  131.8 29.9 %collective-permute-start.11 = (f32[128,1152]{1,0:T(8,128)}, f32[128,1152]{1,0:T(8,128)}, u32[]{:S(2)}, u32[]{:S(2)}) collective-permute-start(f32[128,1152]{1,0:T(8,128)} %collective-permute-done.9.refs_5_), channel_id=1, source_target_pairs={{2,3},{6,7},{10,11},{14,15},{18,19},{22,23},{26,27},{30,31}} | collective-permute-start | bytes 1769480 | tf_op jit(solution)/shard_map/ppermute | solution.py:463
  137.0 24.6 %collective-permute-start.16 = (f32[128,1152]{1,0:T(8,128)}, f32[128,1152]{1,0:T(8,128)}, u32[]{:S(2)}, u32[]{:S(2)}) collective-permute-start(f32[128,1152]{1,0:T(8,128)} %collective-permute-done.14.refs_8_.refs_10_), channel_id=1, source_target_pairs={{1,0},{5,4},{9,8},{13,12},{17,16},{21,20},{25,24},{29,28}} | collective-permute-start | bytes 1769480 | tf_op jit(solution)/shard_map/ppermute | solution.py:464
  181.9 28.9 %collective-permute-start.34 = (f32[512,256]{1,0:T(8,128)S(1)}, f32[512,256]{1,0:T(8,128)S(1)}, u32[]{:S(2)}, u32[]{:S(2)}) collective-permute-start(f32[512,256]{1,0:T(8,128)S(1)} %get-tuple-element.34.refs_3_), channel_id=1, source_target_pairs={{3,2},{7,6},{11,10},{15,14},{19,18},{23,22},{27,26},{31,30}} | collective-permute-start | bytes 1572872 | tf_op jit(solution)/shard_map/ppermute | solution.py:477
  183.2 29.6 %collective-permute-start.31 = (f32[512,256]{1,0:T(8,128)S(1)}, f32[512,256]{1,0:T(8,128)S(1)}, u32[]{:S(2)}, u32[]{:S(2)}) collective-permute-start(f32[512,256]{1,0:T(8,128)S(1)} %get-tuple-element.34.refs_3_), channel_id=1, source_target_pairs={{0,1},{4,5},{8,9},{12,13},{16,17},{20,21},{24,25},{28,29}} | collective-permute-start | bytes 1572872 | tf_op jit(solution)/shard_map/ppermute | solution.py:477
  199.7 25.4 %collective-permute-start.29 = (f32[648,256]{1,0:T(8,128)S(1)}, f32[648,256]{1,0:T(8,128)S(1)}, u32[]{:S(2)}, u32[]{:S(2)}) collective-permute-start(f32[648,256]{1,0:T(8,128)S(1)} %add.32), channel_id=1, source_target_pairs={{2,1},{3,2},{6,5},{7,6},{10,9},{11,10},{14,13},{15,14},{18,17},{19... | collective-permute-start | bytes 1990664 | tf_op jit(solution)/shard_map/ppermute | solution.py:477
  201.7 25.4 %collective-permute-start.26 = (f32[648,256]{1,0:T(8,128)S(1)}, f32[648,256]{1,0:T(8,128)S(1)}, u32[]{:S(2)}, u32[]{:S(2)}) collective-permute-start(f32[648,256]{1,0:T(8,128)S(1)} %add.30), channel_id=1, source_target_pairs={{0,1},{1,2},{4,5},{5,6},{8,9},{9,10},{12,13},{13,14},{16,17},{17,1... | collective-permute-start | bytes 1990664 | tf_op jit(solution)/shard_map/ppermute | solution.py:477
  210.9 25.4 %collective-permute-start.35 = (f32[512,256]{1,0:T(8,128)S(1)}, f32[512,256]{1,0:T(8,128)S(1)}, u32[]{:S(2)}, u32[]{:S(2)}) collective-permute-start(f32[512,256]{1,0:T(8,128)S(1)} %add.36), channel_id=1, source_target_pairs={{2,1},{3,2},{6,5},{7,6},{10,9},{11,10},{14,13},{15,14},{18,17},{19... | collective-permute-start | bytes 1572872 | tf_op jit(solution)/shard_map/ppermute | solution.py:477
  212.9 25.5 %collective-permute-start.32 = (f32[512,256]{1,0:T(8,128)S(1)}, f32[512,256]{1,0:T(8,128)S(1)}, u32[]{:S(2)}, u32[]{:S(2)}) collective-permute-start(f32[512,256]{1,0:T(8,128)S(1)} %add.34), channel_id=1, source_target_pairs={{0,1},{1,2},{4,5},{5,6},{8,9},{9,10},{12,13},{13,14},{16,17},{17,1... | collective-permute-start | bytes 1572872 | tf_op jit(solution)/shard_map/ppermute | solution.py:477
  225.1 25.4 %collective-permute-start.30 = (f32[648,256]{1,0:T(8,128)S(1)}, f32[648,256]{1,0:T(8,128)S(1)}, u32[]{:S(2)}, u32[]{:S(2)}) collective-permute-start(f32[648,256]{1,0:T(8,128)S(1)} %add.33), channel_id=1, source_target_pairs={{1,0},{2,1},{3,2},{5,4},{6,5},{7,6},{9,8},{10,9},{11,10},{13,12},{... | collective-permute-start | bytes 1990664 | tf_op jit(solution)/shard_map/ppermute | solution.py:477
  (44 other events, 837.1 us)
where the time goes:
time: 263 us; the launch traced here: 262 us
  waiting for transfers between devices  136 us (52%)
  starting transfers between devices  62.2 us (24%)
  Pallas kernels  43.6 us (17%)
  local copies, waits for them, and re-layouts  19 us (7%)
    ppermute x6, waiting for transfers between devices, gather_basis(): lax.ppermute(v, 'row', swapped(n_row, b))  48.7 us
    ppermute x12, waiting for transfers between devices, scatter_line(): got[h][way] = lax.ppermute(load, 'col', perm)  45.4 us
    ppermute x6, waiting for transfers between devices, gather_line(): b = [lax.ppermute(x, 'col', left) for x in b]  25.2 us
    ppermute x12, starting transfers between devices, scatter_line(): got[h][way] = lax.ppermute(load, 'col', perm)  22.5 us
    ppermute x6, starting transfers between devices, gather_line(): a = [lax.ppermute(x, 'col', right) for x in a]  17.6 us
    ppermute x6, waiting for transfers between devices, gather_line(): a = [lax.ppermute(x, 'col', right) for x in a]  16.2 us
    unnamed x62, local copies, waits for them, and re-layouts  15.7 us
    ppermute x6, starting transfers between devices, gather_line(): b = [lax.ppermute(x, 'col', left) for x in b]  15.5 us
  transfers between devices with their start and end apart: 37, of which 16 were waited for; matrix products, arithmetic and copies ran while one was open for 1% of the time, Pallas kernels for 12%

commit v1 on v0

--- a/solution.py
+++ b/solution.py
@@ -150,9 +150,9 @@
 def middle_kernel(n, place, *refs):
     reach = n - 1
     grads = by_distance(n, reach, refs[: 4 * reach + 1])
-    acc, s_hi, s_lo, out, r_hi, r_lo, g_all, held, q_hi, q_lo, g_sem, q_sem, out_sem = refs[4 * reach + 1 :]
+    s_hi, s_lo, out, r_hi, r_lo, g_all, held, q_hi, q_lo, g_sem, q_sem, out_sem = refs[4 * reach + 1 :]
     col, pair, skip = place[0], place[1], place[3]
-    brought = [pltpu.make_async_copy(x, y, q_sem.at[k]) for k, (x, y) in enumerate(((s_hi, q_hi), (s_lo, q_lo), (acc, held)))]
+    brought = [pltpu.make_async_copy(x, y, q_sem.at[k]) for k, (x, y) in enumerate(((s_hi, q_hi), (s_lo, q_lo)))]
     start_block(grads, n, pair ^ skip, col, g_all.at[0], g_sem.at[0])
     for copy in brought:
         copy.start()
@@ -164,8 +164,7 @@
     part += jnp.dot(g_lo, q_hi[...], preferred_element_type=f32)
     brought[1].wait()
     part += jnp.dot(g_hi, q_lo[...], preferred_element_type=f32)
-    brought[2].wait()
-    held[...] += part
+    held[...] = part
     sent = pltpu.make_async_copy(held, out, out_sem)
     sent.start()
     landed(g_all.at[1], g_sem.at[1])
@@ -176,10 +175,10 @@
 def rotate_kernel(n, layout, place, *refs):
     count = len(layout)
     pieces = [(*key, ref) for key, ref in zip(layout, refs[:count])]
-    given, refs = refs[count : count + 7], refs[count + 7 :]
+    given, refs = refs[count : count + 8], refs[count + 8 :]
     made, refs = refs[:5], refs[5:]
-    held, refs = refs[:7], refs[7:]
-    acc, g_hi, g_lo, first, second, s_hi, s_lo = held
+    held, refs = refs[:8], refs[8:]
+    part, g_hi, g_lo, first, second, s_hi, s_lo, acc = held
     results, (stage, q_hi, q_lo, p_sem, in_sem, out_sem) = refs[:5], refs[5:]
     nf, ns, d, top, bottom = results
     core, lead = place[2], place[4]
@@ -192,7 +191,7 @@
     for c in range(2):
         landed(stage.at[c], p_sem.at[c])
         if c:
-            for k in (0, 3, 4):
+            for k in (0, 3, 4, 7):
                 brought[k].start()
 
             @pl.when(lead != last)
@@ -207,9 +206,9 @@
     total = jnp.dot(g_hi[...], q_hi[...], preferred_element_type=f32)
     total += jnp.dot(g_hi[...], q_lo[...], preferred_element_type=f32)
     total += jnp.dot(g_lo[...], q_hi[...], preferred_element_type=f32)
-    for k in (0, 3, 4):
+    for k in (0, 3, 4, 7):
         brought[k].wait()
-    total += acc[...]
+    total += acc[...] + part[...]
     nf[...] = 0.9 * first[...] + 0.1 * total
     ns[...] = 0.999 * second[...] + 0.001 * total * total
     d[...] = nf[...] / bias_first / (jnp.sqrt(ns[...] / bias_second) + epsilon)
@@ -280,21 +279,21 @@
     )(place, *grads, *pieces)
 
 
-def middle(place, grads, acc, s_hi, s_lo, n):
-    rows, width = acc.shape
+def middle(place, grads, s_hi, s_lo, n):
+    rows, width = grads[0].shape
     shape = jax.ShapeDtypeStruct
     return pl.pallas_call(
         lambda *refs: middle_kernel(n, *refs),
         out_shape=[shape((rows, width), f32)] + [shape((rows, width), bf16)] * 2,
-        in_specs=[SM] + [ANY] * (len(grads) + 3),
+        in_specs=[SM] + [ANY] * (len(grads) + 2),
         out_specs=[ANY] + [VM] * 2,
         scratch_shapes=[pltpu.VMEM((2, rows, width), f32), pltpu.VMEM((rows, width), f32)]
         + [pltpu.VMEM((width, width), bf16)] * 2
-        + [pltpu.SemaphoreType.DMA((2,)), pltpu.SemaphoreType.DMA((3,)), pltpu.SemaphoreType.DMA],
+        + [pltpu.SemaphoreType.DMA((2,))] * 2 + [pltpu.SemaphoreType.DMA],
         compiler_params=params(VMEM_MIB),
         cost_estimate=cost(1, rows, width),
         name="middle",
-    )(place, *grads, acc, s_hi, s_lo)
+    )(place, *grads, s_hi, s_lo)
 
 
 def rotate(place, keys, pieces, given, n):
@@ -501,8 +500,8 @@
             return [key for key in keys if wanted(key)], [x for key, x in zip(keys, pieces) if wanted(key)]
 
         acc, s_hi, s_lo = early(place, [gradient, *rights[: 2 * n - 4], *lefts[: 2 * n - 4]], *some(lambda key: key[0] < n - 1), n)
-        acc, g_hi, g_lo = middle(place, [gradient, *rights, *lefts], acc, s_hi, s_lo, n)
-        given = [acc, g_hi, g_lo, first_moment, second_moment, s_hi, s_lo]
+        part, g_hi, g_lo = middle(place, [gradient, *rights, *lefts], s_hi, s_lo, n)
+        given = [part, g_hi, g_lo, first_moment, second_moment, s_hi, s_lo, acc]
         new_first, new_second, direction, top, bottom = rotate(place, *some(lambda key: key[0] == n - 1), given, n)
         blocks = back(place, direction, top, bottom, keys, pieces, n)
         new_weights = finish(weights, scatter_line([top, bottom], blocks, n), width * n)

time: 263 us -> 262 us (level)
    unnamed x62 -> x60, local copies, waits for them, and re-layouts: 15.7 us -> 14.7 us
where the time goes in v1:
time: 262 us; the launch traced here: 261 us
  waiting for transfers between devices  136 us (52%)
  starting transfers between devices  62.2 us (24%)
  Pallas kernels  43.8 us (17%)
  local copies, waits for them, and re-layouts  18 us (7%)
    ppermute x6, waiting for transfers between devices, gather_basis(): lax.ppermute(v, 'row', swapped(n_row, b))  48.7 us
    ppermute x12, waiting for transfers between devices, scatter_line(): got[h][way] = lax.ppermute(load, 'col', perm)  45.4 us
    ppermute x6, waiting for transfers between devices, gather_line(): b = [lax.ppermute(x, 'col', left) for x in b]  25.2 us
    ppermute x12, starting transfers between devices, scatter_line(): got[h][way] = lax.ppermute(load, 'col', perm)  22.5 us
    ppermute x6, starting transfers between devices, gather_line(): a = [lax.ppermute(x, 'col', right) for x in a]  17.6 us
    ppermute x6, waiting for transfers between devices, gather_line(): a = [lax.ppermute(x, 'col', right) for x in a]  16.2 us
    ppermute x6, starting transfers between devices, gather_line(): b = [lax.ppermute(x, 'col', left) for x in b]  15.5 us
    unnamed x60, local copies, waits for them, and re-layouts  14.7 us
  transfers between devices with their start and end apart: 37, of which 16 were waited for; matrix products, arithmetic and copies ran while one was open for 1% of the time, Pallas kernels for 12%

profile of v1, /device:TPU:20, one launch (start us, length us, event | category | flops | bytes accessed | tf_op | source)
XLA Modules:
  0.0 261.5 jit_solution(13780207350530669806)
XLA Ops:
  10.5 3.5 %collective-permute-start.7 = (f32[128,1152]{1,0:T(8,128)S(1)}, f32[128,1152]{1,0:T(8,128)S(1)}, u32[]{:S(2)}, u32[]{:S(2)}) collective-permute-start(f32[128,1152]{1,0:T(8,128)S(1)} %get-tuple-element.51), channel_id=1, source_target_pairs={{0,1},{1,2},{2,3},{4,5},{5,6},{6,7},{8,9},{9,10},{10,11},{12,13},{... | collective-permute-start | bytes 1769480 | tf_op jit(solution)/shard_map/ppermute | solution.py:462
  14.0 6.0 %collective-permute-done.12.refs_6_.refs_8_ = f32[128,1152]{1,0:T(8,128)S(1)} collective-permute-done((f32[128,1152]{1,0:T(8,128)S(1)}, f32[128,1152]{1,0:T(8,128)S(1)}, u32[]{:S(2)}, u32[]{:S(2)}) %collective-permute-start.12) | collective-permute-done | bytes 589856 | tf_op jit(solution)/shard_map/ppermute | solution.py:463
  26.7 4.8 %collective-permute-done.13.refs_7_.refs_9_ = f32[128,1152]{1,0:T(8,128)S(1)} collective-permute-done((f32[128,1152]{1,0:T(8,128)S(1)}, f32[128,1152]{1,0:T(8,128)S(1)}, u32[]{:S(2)}, u32[]{:S(2)}) %collective-permute-start.13) | collective-permute-done | bytes 589856 | tf_op jit(solution)/shard_map/ppermute | solution.py:463
  32.1 4.4 %collective-permute-start.15 = (f32[128,1152]{1,0:T(8,128)S(1)}, f32[128,1152]{1,0:T(8,128)}, u32[]{:S(2)}, u32[]{:S(2)}) collective-permute-start(f32[128,1152]{1,0:T(8,128)S(1)} %collective-permute-done.13.refs_7_.refs_9_), channel_id=1, source_target_pairs={{2,1},{1,0},{6,5},{5,4},{10,9},{9,8},{14,13},{13,12},{18,17},{17,1... | collective-permute-start | bytes 1769480 | tf_op jit(solution)/shard_map/ppermute | solution.py:463
  43.8 11.0 %collective-permute-done.15.refs_9_.refs_11_ = f32[128,1152]{1,0:T(8,128)} collective-permute-done((f32[128,1152]{1,0:T(8,128)S(1)}, f32[128,1152]{1,0:T(8,128)}, u32[]{:S(2)}, u32[]{:S(2)}) %collective-permute-start.15) | collective-permute-done | bytes 589856 | tf_op jit(solution)/shard_map/ppermute | solution.py:463
  59.0 4.5 %collective-permute-done.3.refs_16_.refs_12_ = f32[288,1152]{1,0:T(8,128)S(1)} collective-permute-done((f32[288,1152]{1,0:T(8,128)S(1)}, f32[288,1152]{1,0:T(8,128)S(1)}, u32[]{:S(2)}, u32[]{:S(2)}) %collective-permute-start.3) | collective-permute-done | bytes 1327136 | tf_op jit(solution)/shard_map/ppermute | solution.py:448
  63.6 7.7 %collective-permute-done.9.refs_5_ = f32[128,1152]{1,0:T(8,128)} collective-permute-done((f32[128,1152]{1,0:T(8,128)S(1)}, f32[128,1152]{1,0:T(8,128)}, u32[]{:S(2)}, u32[]{:S(2)}) %collective-permute-start.9) | collective-permute-done | bytes 589856 | tf_op jit(solution)/shard_map/ppermute | solution.py:462
  71.2 18.8 %collective-permute-done.20.refs_14_.refs_8_ = f32[288,1152]{1,0:T(8,128)S(1)} collective-permute-done((f32[288,1152]{1,0:T(8,128)S(1)}, f32[288,1152]{1,0:T(8,128)S(1)}, u32[]{:S(2)}, u32[]{:S(2)}) %collective-permute-start.20) | collective-permute-done | bytes 1327136 | tf_op jit(solution)/shard_map/ppermute | solution.py:448
  93.9 8.5 %collective-permute-done.10.refs_6_ = f32[128,1152]{1,0:T(8,128)S(1)} collective-permute-done((f32[128,1152]{1,0:T(8,128)S(1)}, f32[128,1152]{1,0:T(8,128)S(1)}, u32[]{:S(2)}, u32[]{:S(2)}) %collective-permute-start.10) | collective-permute-done | bytes 589856 | tf_op jit(solution)/shard_map/ppermute | solution.py:462
  106.3 15.0 %collective-permute-done.1.refs_1_.refs_10_ = f32[288,1152]{1,0:T(8,128)S(1)} collective-permute-done((f32[288,1152]{1,0:T(8,128)S(1)}, f32[288,1152]{1,0:T(8,128)S(1)}, u32[]{:S(2)}, u32[]{:S(2)}) %collective-permute-start.1) | collective-permute-done | bytes 1327136 | tf_op jit(solution)/shard_map/ppermute | solution.py:448
  121.3 10.5 %collective-permute-done.4.refs_3_.refs_16_ = f32[288,1152]{1,0:T(8,128)} collective-permute-done((f32[288,1152]{1,0:T(8,128)S(1)}, f32[288,1152]{1,0:T(8,128)}, u32[]{:S(2)}, u32[]{:S(2)}) %collective-permute-start.4) | collective-permute-done | bytes 1327136 | tf_op jit(solution)/shard_map/ppermute | solution.py:448
  131.8 5.2 %collective-permute-start.11 = (f32[128,1152]{1,0:T(8,128)}, f32[128,1152]{1,0:T(8,128)}, u32[]{:S(2)}, u32[]{:S(2)}) collective-permute-start(f32[128,1152]{1,0:T(8,128)} %collective-permute-done.9.refs_5_), channel_id=1, source_target_pairs={{2,3},{6,7},{10,11},{14,15},{18,19},{22,23},{26,27},{30,31}} | collective-permute-start | bytes 1769480 | tf_op jit(solution)/shard_map/ppermute | solution.py:462
  149.7 10.9 %early.1 = (f32[256,1152]{1,0:T(8,128)S(1)}, bf16[1152,1152]{1,0:T(8,128)(2,1)}, bf16[1152,1152]{1,0:T(8,128)(2,1)}) custom-call(s32[5]{0:T(128)S(1)} %shard_map.76.refs_0_, f32[256,1152]{1,0:T(8,128)S(1)} %copy-done, f32[128,1152]{1,0:T(8,128)S(1)} %copy-done.9, f32[128,1152]{1,0:T(8,128)S(1)} %copy-done.15, f32[128,1152]{1,0:T(8,128)S(1)} %copy-done.17, ...), custom_call_target="tpu_custom_call" | custom-call | flops 4076863488 | bytes 10616832 | tf_op jit(solution)/shard_map/early/pallas_call | solution.py:264
  160.7 6.1 %middle.1 = (f32[256,1152]{1,0:T(8,128)S(1)}, bf16[256,1152]{1,0:T(8,128)(2,1)S(1)}, bf16[256,1152]{1,0:T(8,128)(2,1)S(1)}) custom-call(s32[5]{0:T(128)S(1)} %shard_map.76.refs_0_, f32[256,1152]{1,0:T(8,128)} %refs_1_.3, f32[128,1152]{1,0:T(8,128)S(1)} %copy-done.10, f32[128,1152]{1,0:T(8,128)S(1)} %copy-done.15, f32[128,1152]{1,0:T(8,128)S(1)} %copy-done.17, ...), custom_call_target="tpu_custom_call" | custom-call | flops 2038431744 | bytes 10616832 | tf_op jit(solution)/shard_map/middle/pallas_call | solution.py:285
  166.9 12.2 %rotate.1 = (f32[256,1152]{1,0:T(8,128)}, f32[256,1152]{1,0:T(8,128)}, f32[256,1152]{1,0:T(8,128)S(1)}, f32[648,256]{1,0:T(8,128)S(1)}, f32[512,256]{1,0:T(8,128)S(1)}) custom-call(s32[5]{0:T(128)S(1)} %shard_map.76.refs_0_, f32[288,1152]{1,0:T(8,128)S(1)} %collective-permute-done.1.refs_1_.refs_10_, f32[288,1152]{1,0:T(8,128)} %collective-permute-done.2.refs_2_.refs_11_, ...), custom_call_target="tpu_custom_call" | custom-call | flops 4076863488 | bytes 10616832 | tf_op jit(solution)/shard_map/rotate/pallas_call | solution.py:303
  183.4 11.2 %back.1 = (f32[648,256]{1,0:T(8,128)S(1)}, f32[512,256]{1,0:T(8,128)S(1)}, f32[648,256]{1,0:T(8,128)S(1)}, f32[512,256]{1,0:T(8,128)S(1)}, f32[648,256]{1,0:T(8,...) custom-call(s32[5]{0:T(128)S(1)} %shard_map.76.refs_0_, ...), custom_call_target="tpu_custom_call" | custom-call | flops 6115295232 | bytes 21233664 | tf_op jit(solution)/shard_map/back/pallas_call | solution.py:367
  194.6 4.3 %collective-permute-done.28 = f32[648,256]{1,0:T(8,128)S(1)} collective-permute-done((f32[648,256]{1,0:T(8,128)S(1)}, f32[648,256]{1,0:T(8,128)S(1)}, u32[]{:S(2)}, u32[]{:S(2)}) %collective-permute-start.28) | collective-permute-done | bytes 663584 | tf_op jit(solution)/shard_map/ppermute | solution.py:476
  202.3 7.8 %collective-permute-done.34 = f32[512,256]{1,0:T(8,128)S(1)} collective-permute-done((f32[512,256]{1,0:T(8,128)S(1)}, f32[512,256]{1,0:T(8,128)S(1)}, u32[]{:S(2)}, u32[]{:S(2)}) %collective-permute-start.34) | collective-permute-done | bytes 524320 | tf_op jit(solution)/shard_map/ppermute | solution.py:476
  213.5 10.8 %collective-permute-done.29 = f32[648,256]{1,0:T(8,128)S(1)} collective-permute-done((f32[648,256]{1,0:T(8,128)S(1)}, f32[648,256]{1,0:T(8,128)S(1)}, u32[]{:S(2)}, u32[]{:S(2)}) %collective-permute-start.29) | collective-permute-done | bytes 663584 | tf_op jit(solution)/shard_map/ppermute | solution.py:476
  226.4 4.0 %collective-permute-start.27 = (f32[648,256]{1,0:T(8,128)S(1)}, f32[648,256]{1,0:T(8,128)S(1)}, u32[]{:S(2)}, u32[]{:S(2)}) collective-permute-start(f32[648,256]{1,0:T(8,128)S(1)} %add.31), channel_id=1, source_target_pairs={{0,1},{1,2},{2,3},{4,5},{5,6},{6,7},{8,9},{9,10},{10,11},{12,13},{... | collective-permute-start | bytes 1990664 | tf_op jit(solution)/shard_map/ppermute | solution.py:476
  230.4 5.1 %collective-permute-done.35 = f32[512,256]{1,0:T(8,128)S(1)} collective-permute-done((f32[512,256]{1,0:T(8,128)S(1)}, f32[512,256]{1,0:T(8,128)S(1)}, u32[]{:S(2)}, u32[]{:S(2)}) %collective-permute-start.35) | collective-permute-done | bytes 524320 | tf_op jit(solution)/shard_map/ppermute | solution.py:476
  237.8 4.0 %collective-permute-start.33 = (f32[512,256]{1,0:T(8,128)S(1)}, f32[512,256]{1,0:T(8,128)S(1)}, u32[]{:S(2)}, u32[]{:S(2)}) collective-permute-start(f32[512,256]{1,0:T(8,128)S(1)} %add.35), channel_id=1, source_target_pairs={{0,1},{1,2},{2,3},{4,5},{5,6},{6,7},{8,9},{9,10},{10,11},{12,13},{... | collective-permute-start | bytes 1572872 | tf_op jit(solution)/shard_map/ppermute | solution.py:476
  241.7 8.0 %collective-permute-done.30.refs_3_ = f32[648,256]{1,0:T(8,128)S(1)} collective-permute-done((f32[648,256]{1,0:T(8,128)S(1)}, f32[648,256]{1,0:T(8,128)S(1)}, u32[]{:S(2)}, u32[]{:S(2)}) %collective-permute-start.30) | collective-permute-done | bytes 663584 | tf_op jit(solution)/shard_map/ppermute | solution.py:476
  250.9 9.3 %collective-permute-done.36.b2 = f32[512,256]{1,0:T(8,128)S(1)} collective-permute-done((f32[512,256]{1,0:T(8,128)S(1)}, f32[512,256]{1,0:T(8,128)S(1)}, u32[]{:S(2)}, u32[]{:S(2)}) %collective-permute-start.36) | collective-permute-done | bytes 524320 | tf_op jit(solution)/shard_map/ppermute | solution.py:476
  (128 shorter events, 66.4 us)
Async XLA Ops:
  4.3 27.7 %collective-permute-start.6 = (f32[128,1152]{1,0:T(8,128)S(1)}, f32[128,1152]{1,0:T(8,128)S(1)}, u32[]{:S(2)}, u32[]{:S(2)}) collective-permute-start(f32[128,1152]{1,0:T(8,128)S(1)} %get-tuple-element.52), channel_id=1, source_target_pairs={{0,1},{1,2},{2,3},{4,5},{5,6},{6,7},{8,9},{9,10},{10,11},{12,13},{... | collective-permute-start | bytes 1769480 | tf_op jit(solution)/shard_map/ppermute | solution.py:462
  10.5 26.8 %collective-permute-start.7 = (f32[128,1152]{1,0:T(8,128)S(1)}, f32[128,1152]{1,0:T(8,128)S(1)}, u32[]{:S(2)}, u32[]{:S(2)}) collective-permute-start(f32[128,1152]{1,0:T(8,128)S(1)} %get-tuple-element.51), channel_id=1, source_target_pairs={{0,1},{1,2},{2,3},{4,5},{5,6},{6,7},{8,9},{9,10},{10,11},{12,13},{... | collective-permute-start | bytes 1769480 | tf_op jit(solution)/shard_map/ppermute | solution.py:462
  25.2 33.9 %collective-permute-start = (f32[288,1152]{1,0:T(8,128)S(1)}, f32[288,1152]{1,0:T(8,128)S(1)}, u32[]{:S(2)}, u32[]{:S(2)}) collective-permute-start(f32[288,1152]{1,0:T(8,128)S(1)} %get-tuple-element.50), channel_id=1, source_target_pairs={{0,8},{4,12},{8,0},{12,4},{16,24},{20,28},{24,16},{28,20},{1,9},{5... | collective-permute-start | bytes 3981320 | tf_op jit(solution)/shard_map/ppermute | solution.py:448
  31.6 32.0 %collective-permute-start.3 = (f32[288,1152]{1,0:T(8,128)S(1)}, f32[288,1152]{1,0:T(8,128)S(1)}, u32[]{:S(2)}, u32[]{:S(2)}) collective-permute-start(f32[288,1152]{1,0:T(8,128)S(1)} %get-tuple-element.49), channel_id=1, source_target_pairs={{0,16},{4,20},{8,24},{12,28},{16,0},{20,4},{24,8},{28,12},{1,17},{... | collective-permute-start | bytes 3981320 | tf_op jit(solution)/shard_map/ppermute | solution.py:448
  43.3 46.7 %collective-permute-start.20 = (f32[288,1152]{1,0:T(8,128)S(1)}, f32[288,1152]{1,0:T(8,128)S(1)}, u32[]{:S(2)}, u32[]{:S(2)}) collective-permute-start(f32[288,1152]{1,0:T(8,128)S(1)} %get-tuple-element.50), channel_id=1, source_target_pairs={{0,16},{4,20},{8,24},{12,28},{16,0},{20,4},{24,8},{28,12},{1,17},{... | collective-permute-start | bytes 3981320 | tf_op jit(solution)/shard_map/ppermute | solution.py:448
  57.5 34.8 %collective-permute-start.23 = (f32[288,1152]{1,0:T(8,128)S(1)}, f32[288,1152]{1,0:T(8,128)S(1)}, u32[]{:S(2)}, u32[]{:S(2)}) collective-permute-start(f32[288,1152]{1,0:T(8,128)S(1)} %get-tuple-element.49), channel_id=1, source_target_pairs={{0,8},{4,12},{8,0},{12,4},{16,24},{20,28},{24,16},{28,20},{1,9},{5... | collective-permute-start | bytes 3981320 | tf_op jit(solution)/shard_map/ppermute | solution.py:448
  59.0 45.7 %collective-permute-start.19 = (f32[288,1152]{1,0:T(8,128)S(1)}, f32[288,1152]{1,0:T(8,128)S(1)}, u32[]{:S(2)}, u32[]{:S(2)}) collective-permute-start(f32[288,1152]{1,0:T(8,128)S(1)} %collective-permute-done.refs_12_.refs_6_), channel_id=1, source_target_pairs={{0,4},{4,0},{8,12},{12,8},{16,20},{20,16},{24,28},{28,24},{1,5},{5... | collective-permute-start | bytes 3981320 | tf_op jit(solution)/shard_map/ppermute | solution.py:442
  63.6 42.3 %collective-permute-start.22 = (f32[288,1152]{1,0:T(8,128)S(1)}, f32[288,1152]{1,0:T(8,128)S(1)}, u32[]{:S(2)}, u32[]{:S(2)}) collective-permute-start(f32[288,1152]{1,0:T(8,128)S(1)} %collective-permute-done.3.refs_16_.refs_12_), channel_id=1, source_target_pairs={{0,4},{4,0},{8,12},{12,8},{16,20},{20,16},{24,28},{28,24},{1,5},{5... | collective-permute-start | bytes 3981320 | tf_op jit(solution)/shard_map/ppermute | solution.py:442
  71.2 67.3 %collective-permute-start.18 = (f32[576,1152]{1,0:T(8,128)S(1)}, f32[576,1152]{1,0:T(8,128)S(1)}, u32[]{:S(2)}, u32[]{:S(2)}) collective-permute-start(f32[576,1152]{1,0:T(8,128)S(1)} %copy-done.22), channel_id=1, source_target_pairs={{0,4},{4,0},{8,12},{12,8},{16,20},{20,16},{24,28},{28,24},{1,5},{5... | collective-permute-start | bytes 7962632 | tf_op jit(solution)/shard_map/ppermute | solution.py:442
  92.3 29.0 %collective-permute-start.1 = (f32[288,1152]{1,0:T(8,128)S(1)}, f32[288,1152]{1,0:T(8,128)S(1)}, u32[]{:S(2)}, u32[]{:S(2)}) collective-permute-start(f32[288,1152]{1,0:T(8,128)S(1)} %collective-permute-done.refs_12_.refs_6_), channel_id=1, source_target_pairs={{0,16},{4,20},{8,24},{12,28},{16,0},{20,4},{24,8},{28,12},{1,17},{... | collective-permute-start | bytes 3981320 | tf_op jit(solution)/shard_map/ppermute | solution.py:448
  103.3 28.5 %collective-permute-start.4 = (f32[288,1152]{1,0:T(8,128)S(1)}, f32[288,1152]{1,0:T(8,128)}, u32[]{:S(2)}, u32[]{:S(2)}) collective-permute-start(f32[288,1152]{1,0:T(8,128)S(1)} %collective-permute-done.3.refs_16_.refs_12_), channel_id=1, source_target_pairs={{0,8},{4,12},{8,0},{12,4},{16,24},{20,28},{24,16},{28,20},{1,9},{5... | collective-permute-start | bytes 3981320 | tf_op jit(solution)/shard_map/ppermute | solution.py:448
  105.8 26.0 %collective-permute-start.21 = (f32[288,1152]{1,0:T(8,128)S(1)}, f32[288,1152]{1,0:T(8,128)S(1)}, u32[]{:S(2)}, u32[]{:S(2)}) collective-permute-start(f32[288,1152]{1,0:T(8,128)S(1)} %collective-permute-done.20.refs_14_.refs_8_), channel_id=1, source_target_pairs={{0,4},{4,0},{8,12},{12,8},{16,20},{20,16},{24,28},{28,24},{1,5},{5... | collective-permute-start | bytes 3981320 | tf_op jit(solution)/shard_map/ppermute | solution.py:442
  105.8 31.2 %collective-permute-start.24 = (f32[288,1152]{1,0:T(8,128)S(1)}, f32[288,1152]{1,0:T(8,128)S(1)}, u32[]{:S(2)}, u32[]{:S(2)}) collective-permute-start(f32[288,1152]{1,0:T(8,128)S(1)} %collective-permute-done.23.refs_18_.refs_14_), channel_id=1, source_target_pairs={{0,4},{4,0},{8,12},{12,8},{16,20},{20,16},{24,28},{28,24},{1,5},{5... | collective-permute-start | bytes 3981320 | tf_op jit(solution)/shard_map/ppermute | solution.py:442
  121.3 45.6 %collective-permute-start.2 = (f32[288,1152]{1,0:T(8,128)S(1)}, f32[288,1152]{1,0:T(8,128)}, u32[]{:S(2)}, u32[]{:S(2)}) collective-permute-start(f32[288,1152]{1,0:T(8,128)S(1)} %collective-permute-done.1.refs_1_.refs_10_), channel_id=1, source_target_pairs={{0,4},{4,0},{8,12},{12,8},{16,20},{20,16},{24,28},{28,24},{1,5},{5... | collective-permute-start | bytes 3981320 | tf_op jit(solution)/shard_map/ppermute | solution.py:442
  131.8 35.1 %collective-permute-start.5 = (f32[288,1152]{1,0:T(8,128)}, f32[288,1152]{1,0:T(8,128)}, u32[]{:S(2)}, u32[]{:S(2)}) collective-permute-start(f32[288,1152]{1,0:T(8,128)} %collective-permute-done.4.refs_3_.refs_16_), channel_id=1, source_target_pairs={{0,4},{4,0},{8,12},{12,8},{16,20},{20,16},{24,28},{28,24},{1,5},{5... | collective-permute-start | bytes 3981320 | tf_op jit(solution)/shard_map/ppermute | solution.py:442
  131.8 28.8 %collective-permute-start.11 = (f32[128,1152]{1,0:T(8,128)}, f32[128,1152]{1,0:T(8,128)}, u32[]{:S(2)}, u32[]{:S(2)}) collective-permute-start(f32[128,1152]{1,0:T(8,128)} %collective-permute-done.9.refs_5_), channel_id=1, source_target_pairs={{2,3},{6,7},{10,11},{14,15},{18,19},{22,23},{26,27},{30,31}} | collective-permute-start | bytes 1769480 | tf_op jit(solution)/shard_map/ppermute | solution.py:462
  181.2 28.9 %collective-permute-start.34 = (f32[512,256]{1,0:T(8,128)S(1)}, f32[512,256]{1,0:T(8,128)S(1)}, u32[]{:S(2)}, u32[]{:S(2)}) collective-permute-start(f32[512,256]{1,0:T(8,128)S(1)} %get-tuple-element.34.refs_3_), channel_id=1, source_target_pairs={{3,2},{7,6},{11,10},{15,14},{19,18},{23,22},{27,26},{31,30}} | collective-permute-start | bytes 1572872 | tf_op jit(solution)/shard_map/ppermute | solution.py:476
  182.5 29.6 %collective-permute-start.31 = (f32[512,256]{1,0:T(8,128)S(1)}, f32[512,256]{1,0:T(8,128)S(1)}, u32[]{:S(2)}, u32[]{:S(2)}) collective-permute-start(f32[512,256]{1,0:T(8,128)S(1)} %get-tuple-element.34.refs_3_), channel_id=1, source_target_pairs={{0,1},{4,5},{8,9},{12,13},{16,17},{20,21},{24,25},{28,29}} | collective-permute-start | bytes 1572872 | tf_op jit(solution)/shard_map/ppermute | solution.py:476
  198.9 25.4 %collective-permute-start.29 = (f32[648,256]{1,0:T(8,128)S(1)}, f32[648,256]{1,0:T(8,128)S(1)}, u32[]{:S(2)}, u32[]{:S(2)}) collective-permute-start(f32[648,256]{1,0:T(8,128)S(1)} %add.32), channel_id=1, source_target_pairs={{2,1},{3,2},{6,5},{7,6},{10,9},{11,10},{14,13},{15,14},{18,17},{19... | collective-permute-start | bytes 1990664 | tf_op jit(solution)/shard_map/ppermute | solution.py:476
  201.0 25.4 %collective-permute-start.26 = (f32[648,256]{1,0:T(8,128)S(1)}, f32[648,256]{1,0:T(8,128)S(1)}, u32[]{:S(2)}, u32[]{:S(2)}) collective-permute-start(f32[648,256]{1,0:T(8,128)S(1)} %add.30), channel_id=1, source_target_pairs={{0,1},{1,2},{4,5},{5,6},{8,9},{9,10},{12,13},{13,14},{16,17},{17,1... | collective-permute-start | bytes 1990664 | tf_op jit(solution)/shard_map/ppermute | solution.py:476
  210.2 25.4 %collective-permute-start.35 = (f32[512,256]{1,0:T(8,128)S(1)}, f32[512,256]{1,0:T(8,128)S(1)}, u32[]{:S(2)}, u32[]{:S(2)}) collective-permute-start(f32[512,256]{1,0:T(8,128)S(1)} %add.36), channel_id=1, source_target_pairs={{2,1},{3,2},{6,5},{7,6},{10,9},{11,10},{14,13},{15,14},{18,17},{19... | collective-permute-start | bytes 1572872 | tf_op jit(solution)/shard_map/ppermute | solution.py:476
  212.2 25.5 %collective-permute-start.32 = (f32[512,256]{1,0:T(8,128)S(1)}, f32[512,256]{1,0:T(8,128)S(1)}, u32[]{:S(2)}, u32[]{:S(2)}) collective-permute-start(f32[512,256]{1,0:T(8,128)S(1)} %add.34), channel_id=1, source_target_pairs={{0,1},{1,2},{4,5},{5,6},{8,9},{9,10},{12,13},{13,14},{16,17},{17,1... | collective-permute-start | bytes 1572872 | tf_op jit(solution)/shard_map/ppermute | solution.py:476
  224.4 25.4 %collective-permute-start.30 = (f32[648,256]{1,0:T(8,128)S(1)}, f32[648,256]{1,0:T(8,128)S(1)}, u32[]{:S(2)}, u32[]{:S(2)}) collective-permute-start(f32[648,256]{1,0:T(8,128)S(1)} %add.33), channel_id=1, source_target_pairs={{1,0},{2,1},{3,2},{5,4},{6,5},{7,6},{9,8},{10,9},{11,10},{13,12},{... | collective-permute-start | bytes 1990664 | tf_op jit(solution)/shard_map/ppermute | solution.py:476
  235.6 24.6 %collective-permute-start.36 = (f32[512,256]{1,0:T(8,128)S(1)}, f32[512,256]{1,0:T(8,128)S(1)}, u32[]{:S(2)}, u32[]{:S(2)}) collective-permute-start(f32[512,256]{1,0:T(8,128)S(1)} %add.37), channel_id=1, source_target_pairs={{1,0},{2,1},{3,2},{5,4},{6,5},{7,6},{9,8},{10,9},{11,10},{13,12},{... | collective-permute-start | bytes 1572872 | tf_op jit(solution)/shard_map/ppermute | solution.py:476
  (43 other events, 830.1 us)
